TPU v7x, 32 devices: a whole 2x2x4 slice. The times are simulated.
32 devices in a mesh: ao: 8 (over y, x, core), aux: 4 (over z).
Axes of the slice: x: 2, y: 2, z: 4, core: 2. Of those that a mesh axis runs over, the one named last changes fastest.
Arguments:
- blocks: bfloat16 [48, 256, 128, 128], P('ao', 'aux'), may hold values from -6 to 6
- pairs: int32 [48, 2], P('ao'), may hold values from 0 to 79, as said below
- counts: int32 [8], P('ao'), may hold values from 1 to 6, as said below
- owned_blocks: int32 [80], P('ao'), may hold values from 0 to 79, as said below
- occ_coef: bfloat16 [80, 8, 128], P('ao'), may hold values from -0.5 to 0.5
- vir_coef: bfloat16 [10240, 9216], P('ao', 'aux'), may hold values from -0.109375 to 0.109375
Outputs:
- b_tensor: bfloat16 [256, 8, 9216], P('ao', None, 'aux')
Inputs may be any that keep to these rules, and one draw needn't show every extreme that they name: `pairs`: among the used slots of one ao index, at most 3 have nu blocks whose rows one owner holds; in every draw some index reaches 3. `counts`: some ao index uses all 6 slots in every draw. `owned_blocks`: every atom block appears exactly once.
All inputs are finite; a program needn't handle non-finite values.
Results may differ from a plain program's by a relative error of at most 0.014.
Values may be sent and summed in bfloat16 or wider, within the bound.
A program may use at most 128 MiB of HBM per device.

v0:
```python
import functools

import jax
import jax.numpy as jnp
from jax import lax
from jax.experimental import pallas as pl
from jax.experimental.pallas import tpu as pltpu
from jax.sharding import PartitionSpec as P

MESH = pl.DeviceIdType.MESH
CAP = 3
CHUNKS = 4


def few_blocks(per_owner):
    return -(-per_owner * 2 // 3)


def block_place(block_ids, owned_all):
    hits = block_ids[..., None] == owned_all
    positions = jnp.arange(owned_all.shape[0], dtype=jnp.int32)
    return jnp.sum(jnp.where(hits, positions, 0), axis=-1)


def small_kernel(n, meta_ref, occ_ref, meta_out, occ_out, s_sem, r_sem, l_sem):
    me = lax.axis_index("ao")
    barrier = pltpu.get_barrier_semaphore()
    for k in range(1, n):
        pl.semaphore_signal(barrier, inc=1, device_id={"ao": lax.rem(me + k, n)}, device_id_type=MESH)
    own = [
        pltpu.make_async_copy(meta_ref, meta_out.at[me], l_sem.at[0]),
        pltpu.make_async_copy(occ_ref, occ_out.at[me], l_sem.at[1]),
    ]
    for copy in own:
        copy.start()
    pl.semaphore_wait(barrier, n - 1)
    sent = []
    for k in range(1, n):
        for which, (src, dst) in enumerate(((meta_ref, meta_out), (occ_ref, occ_out))):
            copy = pltpu.make_async_remote_copy(
                src_ref=src, dst_ref=dst.at[me], send_sem=s_sem.at[which, k], recv_sem=r_sem.at[which, k],
                device_id={"ao": lax.rem(me + k, n)}, device_id_type=MESH,
            )
            copy.start()
            sent.append(copy)
    for copy in own + sent:
        copy.wait()


def gather_small(n, meta, occ):
    return pl.pallas_call(
        functools.partial(small_kernel, n),
        out_shape=(
            jax.ShapeDtypeStruct((n,) + meta.shape, meta.dtype),
            jax.ShapeDtypeStruct((n,) + occ.shape, occ.dtype),
        ),
        in_specs=[pl.BlockSpec(memory_space=pltpu.VMEM)] * 2,
        out_specs=(pl.BlockSpec(memory_space=pltpu.VMEM),) * 2,
        scratch_shapes=[
            pltpu.SemaphoreType.DMA((2, n)),
            pltpu.SemaphoreType.DMA((2, n)),
            pltpu.SemaphoreType.DMA((2,)),
        ],
        compiler_params=pltpu.CompilerParams(collective_id=0, has_side_effects=True),
    )(meta, occ)


def main_kernel(
    n, nz, kept, idx_ref, w_ref, pick_ref, half_ref, vir_hbm, out_ref,
    vir_all, vir, snd, rcv, rows, part, pair, rx, ry, tx, ty,
    vir_sem, own_sem, a_s, a_r, up_s, up_r, dn_s, dn_r, p_s, p_r, x_s, x_r, y_s, y_r,
):
    me, z = lax.axis_index("ao"), lax.axis_index("aux")
    core, chip = lax.rem(me, 2), me // 2
    cx, cy = lax.rem(chip, 2), chip // 2
    mate = me + 1 - 2 * core
    xmate = me + 2 - 4 * cx
    ymate = me + 4 - 8 * cy
    total = n * CAP
    width = rcv.shape[-1]
    step = rcv.shape[3]
    mid = step // 2

    barrier = pltpu.get_barrier_semaphore()
    for k in range(1, n):
        pl.semaphore_signal(barrier, inc=1, device_id={"ao": lax.rem(me + k, n)}, device_id_type=MESH)
    for k in range(1, nz):
        pl.semaphore_signal(barrier, inc=1, device_id={"aux": lax.rem(z + k, nz)}, device_id_type=MESH)
    vir_copy = pltpu.make_async_copy(vir_hbm, vir_all, vir_sem)
    vir_copy.start()

    def pack(i, carry):
        snd[i] = half_ref[idx_ref[i]]
        return carry

    lax.fori_loop(0, total, pack, 0)
    pl.semaphore_wait(barrier, n + nz - 2)

    a_copies = []
    for c in range(CHUNKS):
        span = pl.ds(c * step, step)
        mine = pl.ds(me * CAP, CAP)
        local = pltpu.make_async_copy(snd.at[mine, :, span, :], rcv.at[c, mine], own_sem.at[c])
        local.start()
        group = [local]
        for k in range(1, n):
            dst = lax.rem(me + k, n)
            copy = pltpu.make_async_remote_copy(
                src_ref=snd.at[pl.ds(dst * CAP, CAP), :, span, :], dst_ref=rcv.at[c, mine],
                send_sem=a_s.at[c, k], recv_sem=a_r.at[c, k],
                device_id={"ao": dst}, device_id_type=MESH,
            )
            copy.start()
            group.append(copy)
        a_copies.append(group)

    def z_copy(c, d, up):
        src = z - d if up else z + d
        return pltpu.make_async_remote_copy(
            src_ref=rows.at[c, src], dst_ref=rows.at[c, src],
            send_sem=(up_s if up else dn_s).at[c, d], recv_sem=(up_r if up else dn_r).at[c, d],
            device_id={"aux": z + 1 if up else z - 1}, device_id_type=MESH,
        )

    def z_send(c, d):
        @pl.when((z - d >= 0) & (z + 1 < nz))
        def _():
            z_copy(c, d, True).start()

        @pl.when((z + d < nz) & (z >= 1))
        def _():
            z_copy(c, d, False).start()

    def z_recv(c, d, up):
        src = z - d if up else z + d
        return pltpu.make_async_remote_copy(
            src_ref=rows.at[c, src], dst_ref=rows.at[c, src],
            send_sem=(up_s if up else dn_s).at[c, d - 1], recv_sem=(up_r if up else dn_r).at[c, d - 1],
            device_id={"aux": z - 1 if up else z + 1}, device_id_type=MESH,
        )

    def stage_a(c):
        a_copies[c][0].wait()
        for copy in a_copies[c][1:]:
            copy.wait_recv()
        for l in range(kept):
            def add(s, acc):
                for j in range(CAP):
                    t = s * CAP + j
                    acc = acc + w_ref[l * total + t] * rcv[c, t].astype(jnp.float32)
                return acc

            acc = lax.fori_loop(0, n, add, jnp.zeros((2, step, width), jnp.float32))
            rows[c, z, :, l * width:(l + 1) * width] = acc.reshape(2 * step, width).astype(jnp.bfloat16)
        z_send(c, 0)

    def stage_b(c, d):
        @pl.when(z - d >= 0)
        def _():
            z_recv(c, d, True).wait_recv()

        @pl.when(z + d < nz)
        def _():
            z_recv(c, d, False).wait_recv()

        if d < nz - 1:
            z_send(c, d)

    pair_copies, x_copies, y_copies = {}, {}, {}

    def remote(src, dst, ss, rs, to):
        copy = pltpu.make_async_remote_copy(
            src_ref=src, dst_ref=dst, send_sem=ss, recv_sem=rs, device_id={"ao": to}, device_id_type=MESH,
        )
        copy.start()
        return copy

    tile = 256
    depth = rows.shape[-1]

    def stage_m(c):
        @pl.loop(0, vir.shape[1] // tile)
        def _(j):
            cols = pl.ds(pl.multiple_of(j * tile, tile), tile)
            left = rows[c].reshape(nz * 2 * step, depth)
            got = jnp.dot(left, vir[:, cols], preferred_element_type=jnp.float32)
            got = got.astype(jnp.bfloat16).reshape(nz, 2, step, tile)
            for h in range(2):
                part[c, h, :, :, cols] = got[:, h]

        pair_copies[c] = remote(part.at[c, 1 - core], pair.at[c], p_s.at[c], p_r.at[c], mate)

    def add2(a, b):
        return (a.astype(jnp.float32) + b.astype(jnp.float32)).astype(jnp.bfloat16)

    def stage_p(c):
        pair_copies[c].wait_recv()

        @pl.loop(0, nz)
        def _(i):
            pair[c, i] = add2(pair[c, i], part[c, core, i])

        lo, hi = pl.ds(0, mid), pl.ds(mid, mid)
        x_copies[c] = [
            remote(pair.at[c, 1 - cx, lo], rx.at[c, 0], x_s.at[c, 0], x_r.at[c, 0], xmate),
            remote(pair.at[c, 2 * (1 - cy), hi], ry.at[c, 0], y_s.at[c, 0], y_r.at[c, 0], ymate),
            remote(pair.at[c, 3 - cx, lo], rx.at[c, 1], x_s.at[c, 1], x_r.at[c, 1], xmate),
            remote(pair.at[c, 2 * (1 - cy) + 1, hi], ry.at[c, 1], y_s.at[c, 1], y_r.at[c, 1], ymate),
        ]

    def stage_x(c):
        for copy in x_copies[c]:
            copy.wait_recv()
        tx[c] = add2(pair[c, 2 * (1 - cy) + cx, :mid], rx[c, 1 - cy])
        ty[c] = add2(pair[c, 2 * cy + 1 - cx, mid:], ry[c, 1 - cx])
        y_copies[c] = [
            remote(tx.at[c], rx.at[c, 2], y_s.at[c, 2], y_r.at[c, 2], ymate),
            remote(ty.at[c], ry.at[c, 2], x_s.at[c, 2], x_r.at[c, 2], xmate),
        ]

    def stage_y(c):
        for copy in y_copies[c]:
            copy.wait_recv()
        f32 = jnp.float32
        own = pair[c, 2 * cy + cx]
        top = own[:mid].astype(f32) + rx[c, cy].astype(f32) + rx[c, 2].astype(f32)
        low = own[mid:].astype(f32) + ry[c, cx].astype(f32) + ry[c, 2].astype(f32)
        out_ref[c * step:c * step + mid, :] = top.astype(jnp.bfloat16)
        out_ref[c * step + mid:(c + 1) * step, :] = low.astype(jnp.bfloat16)

    vir_copy.wait()
    piece = 16

    @pl.loop(0, width // piece)
    def _(i):
        at = pl.ds(pl.multiple_of(i * piece, piece), piece)
        for k in range(kept):
            to = pl.ds(pl.multiple_of(k * width + i * piece, piece), piece)
            vir[to, :] = vir_all[pick_ref[k], at, :]

    plan = (
        "A0 B01 A1 B02", "A2 B11 B03 M0", "A3 B12 B21 P0", "B13 M1 B22 B31",
        "X0 P1 B23 M2", "B32 Y0 X1 P2", "B33 M3 Y1 X2", "P3 Y2 X3 Y3",
    )
    run = {"A": stage_a, "B": stage_b, "M": stage_m, "P": stage_p, "X": stage_x, "Y": stage_y}
    for item in [name for row in plan for name in row.split()]:
        run[item[0]](*[int(v) for v in item[1:]])

    for c in range(CHUNKS):
        for copy in a_copies[c][1:] + [pair_copies[c]] + x_copies[c] + y_copies[c]:
            copy.wait_send()
        for d in range(nz - 1):
            @pl.when((z - d >= 0) & (z + 1 < nz))
            def _():
                z_copy(c, d, True).wait_send()

            @pl.when((z + d < nz) & (z >= 1))
            def _():
                z_copy(c, d, False).wait_send()


def fused(n, nz, kept, call_id, idx, weights, pick, half, vir_coef):
    _, _, span, width = half.shape
    step = span // CHUNKS
    columns = vir_coef.shape[2]
    bf = jnp.bfloat16
    dma = pltpu.SemaphoreType.DMA
    vm = pltpu.VMEM
    return pl.pallas_call(
        functools.partial(main_kernel, n, nz, kept),
        out_shape=jax.ShapeDtypeStruct((span, columns), bf),
        in_specs=[
            pl.BlockSpec(memory_space=pltpu.SMEM),
            pl.BlockSpec(memory_space=pltpu.SMEM),
            pl.BlockSpec(memory_space=pltpu.SMEM),
            pl.BlockSpec(memory_space=pltpu.VMEM),
            pl.BlockSpec(memory_space=pl.ANY),
        ],
        out_specs=pl.BlockSpec(memory_space=pltpu.VMEM),
        scratch_shapes=[
            vm(vir_coef.shape, bf),
            vm((kept * width, columns), bf),
            vm((n * CAP, 2, span, width), bf),
            vm((CHUNKS, n * CAP, 2, step, width), bf),
            vm((CHUNKS, nz, 2 * step, kept * width), bf),
            vm((CHUNKS, 2, nz, step, columns), bf),
            vm((CHUNKS, nz, step, columns), bf),
            vm((CHUNKS, 3, step // 2, columns), bf),
            vm((CHUNKS, 3, step // 2, columns), bf),
            vm((CHUNKS, step // 2, columns), bf),
            vm((CHUNKS, step // 2, columns), bf),
            dma, dma((CHUNKS,)),
            dma((CHUNKS, n)), dma((CHUNKS, n)),
            dma((CHUNKS, nz)), dma((CHUNKS, nz)), dma((CHUNKS, nz)), dma((CHUNKS, nz)),
            dma((CHUNKS,)), dma((CHUNKS,)),
            dma((CHUNKS, 3)), dma((CHUNKS, 3)), dma((CHUNKS, 3)), dma((CHUNKS, 3)),
        ],
        compiler_params=pltpu.CompilerParams(
            collective_id=call_id, has_side_effects=True, vmem_limit_bytes=62 * 1024 * 1024,
        ),
    )(idx, weights, pick, half, vir_coef)


def per_device(blocks, pairs, counts, owned_blocks, occ_coef, vir_coef):
    groups, nz = lax.axis_size("ao"), lax.axis_size("aux")
    me = lax.axis_index("ao")
    slots, aux_depth, _, width = blocks.shape
    per_owner, occupied, _ = occ_coef.shape
    flat = jnp.concatenate([pairs.reshape(-1), counts, owned_blocks])
    used = flat.shape[0]
    meta = jnp.broadcast_to(jnp.pad(flat, (0, -used % 128))[None], (8, used + -used % 128))
    meta_all, occ_all = gather_small(groups, meta, occ_coef.reshape(per_owner * occupied, width))
    meta_all = meta_all[:, 0]
    all_pairs = meta_all[:, :2 * slots].reshape(groups, slots, 2)
    all_counts = meta_all[:, 2 * slots]
    all_owned = meta_all[:, 2 * slots + 1:used].reshape(-1)
    occ_all = occ_all.reshape(groups * per_owner, occupied, width)

    slot_ids = jnp.arange(slots, dtype=jnp.int32)
    in_use = slot_ids < counts[0]
    occ_pick = occ_all[block_place(pairs[:, 0], all_owned)]
    half = jnp.einsum("sim,spmn->spin", occ_pick, blocks, preferred_element_type=jnp.float32)
    half = jnp.where(in_use[:, None, None, None], half, 0.0).astype(jnp.bfloat16)
    half = half.reshape(slots, 2, aux_depth * occupied // 2, width)

    place = block_place(all_pairs[:, :, 1], all_owned)
    live = slot_ids[None, :] < all_counts[:, None]
    owner, local = place // per_owner, place % per_owner
    same = (owner[:, :, None] == owner[:, None, :]) & live[:, None, :]
    rank = jnp.sum(jnp.where(same & (slot_ids[None, None, :] < slot_ids[None, :, None]), 1, 0), axis=-1)
    ranks = jnp.arange(CAP, dtype=jnp.int32)
    mine = live & (owner == me)
    positions = jnp.arange(per_owner, dtype=jnp.int32)
    hit = live[None, None] & (place[None, None] == (
        jnp.arange(groups, dtype=jnp.int32)[:, None] * per_owner + positions)[:, :, None, None])
    seen = jnp.any(hit, axis=(2, 3))
    most = jnp.max(jnp.sum(jnp.where(seen, 1, 0), axis=1))
    my_seen = jnp.any(mine[None] & (local[None] == positions[:, None, None]), axis=(1, 2))
    order = jnp.sum(jnp.where(my_seen[None, :] & (positions[None, :] < positions[:, None]), 1, 0), axis=1)
    listed = my_seen[None, :] & (order[None, :] == positions[:, None])
    pick = jnp.sum(jnp.where(listed, positions[None, :], 0), axis=1)
    spot = jnp.sum(jnp.where(local[:, :, None] == positions, order, 0), axis=-1)
    weights = (
        mine[None, :, None, :]
        & (spot[None, :, None, :] == positions[:, None, None, None])
        & (rank[None, :, None, :] == ranks[None, None, :, None])
    )
    weights = jnp.sum(jnp.where(weights, 1.0, 0.0), axis=-1).reshape(-1)
    my_owner, my_live, my_rank = (jnp.take(v, me, axis=0) for v in (owner, live, rank))
    chosen = (
        my_live[None, None, :]
        & (my_owner[None, None, :] == jnp.arange(groups, dtype=jnp.int32)[:, None, None])
        & (my_rank[None, None, :] == ranks[None, :, None])
    )
    idx = jnp.sum(jnp.where(chosen, slot_ids, 0), axis=-1).reshape(-1)
    few = few_blocks(per_owner)
    vir3 = vir_coef.reshape(per_owner, width, vir_coef.shape[1])
    out = lax.cond(
        most <= few,
        functools.partial(fused, groups, nz, few, 1),
        functools.partial(fused, groups, nz, per_owner, 2),
        idx, weights, pick, half, vir3,
    )
    return out.reshape(-1, occupied, vir_coef.shape[1])


def per_device_general(blocks, pairs, counts, owned_blocks, occ_coef, vir_coef):
    groups = lax.axis_size("ao")
    own_index = lax.axis_index("ao")
    slot_count = blocks.shape[0]
    aux_depth = blocks.shape[1]
    block_width = blocks.shape[3]
    occupied = occ_coef.shape[1]
    all_pairs, all_counts, all_owned = (
        lax.all_gather(pairs, "ao", axis=0, tiled=True),
        lax.all_gather(counts, "ao", axis=0, tiled=True),
        lax.all_gather(owned_blocks, "ao", axis=0, tiled=True),
    )
    occ_all = lax.all_gather(occ_coef, "ao", axis=0, tiled=True)
    per_owner = all_owned.shape[0] // groups
    slot_ids = jnp.arange(slot_count, dtype=jnp.int32)
    in_use = slot_ids < counts[0]
    occ_pick = occ_all[block_place(pairs[:, 0], all_owned)]
    slab_values = jnp.einsum("sim,spmn->spin", occ_pick, blocks, preferred_element_type=jnp.float32)
    slab_values = jnp.where(in_use[:, None, None, None], slab_values, 0.0).astype(jnp.bfloat16)
    flat_slabs = slab_values.reshape(slot_count, aux_depth * occupied, block_width)
    place_all = block_place(all_pairs[:, 1], all_owned).reshape(groups, slot_count)
    owner_all = place_all // per_owner
    local_all = place_all % per_owner
    live_all = slot_ids[None, :] < all_counts[:, None]
    mine_all = live_all & (owner_all == own_index)
    local_ids = jnp.arange(per_owner, dtype=jnp.int32)
    slabs_got = lax.all_gather(flat_slabs, "ao", axis=0, tiled=True)
    assign = (
        mine_all.reshape(-1)[None, :] & (local_all.reshape(-1)[None, :] == local_ids[:, None])
    ).astype(jnp.bfloat16)
    summed = jnp.einsum("lt,tqm->qlm", assign, slabs_got, preferred_element_type=jnp.float32)
    rows_local = summed.reshape(summed.shape[0], per_owner * block_width).astype(jnp.bfloat16)
    rows_whole = lax.all_gather(rows_local, "aux", axis=0, tiled=True)
    share = rows_whole.shape[0] // groups
    result = lax.psum_scatter(
        jnp.dot(rows_whole, vir_coef, preferred_element_type=jnp.float32).astype(jnp.bfloat16),
        "ao",
        scatter_dimension=0,
        tiled=True,
    )
    return result.reshape(share // occupied, occupied, vir_coef.shape[1])


def solution(mesh):
    in_specs = (
        P("ao", "aux", None, None),
        P("ao", None),
        P("ao"),
        P("ao"),
        P("ao", None, None),
        P("ao", "aux"),
    )
    out_specs = P("ao", None, "aux")
    small = mesh.shape["ao"] == 8 and mesh.shape["aux"] == 4
    body = per_device if small else per_device_general
    return jax.shard_map(body, mesh=mesh, in_specs=in_specs, out_specs=out_specs, check_vma=False)
```

profile of v0, /device:TPU:0, one launch (start us, length us, event | category | flops | bytes accessed | tf_op | source)
XLA Modules:
  0.0 132.5 jit_solution(7763353427875726120)
XLA Ops:
  0.7 0.7 slice_bitcast_fusion
  1.4 0.8 copy.90
  2.3 0.7 pad_add_fusion
  3.0 0.6 broadcast_in_dim.173.meta_ref
  3.7 9.0 %shard_map.72 = (s32[8,8,128]{2,1,0:T(8,128)}, bf16[8,80,128]{2,1,0:T(8,128)(2,1)}) custom-call(s32[8,128]{1,0:T(8,128)} %broadcast_in_dim.173.meta_ref, bf16[80,128]{1,0:T(8,128)(2,1)} %bitcast.79), custom_call_target="tpu_custom_call" | custom-call | tf_op jit(solution)/shard_map/pallas_call | solution.py:51
  12.7 0.8 slice.18
  13.5 0.2 slice_reduce_fusion
  13.8 0.2 select_reduce_fusion.14
  14.0 1.5 %gather_fusion = bf16[6,8,128]{2,1,0:T(8,128)(2,1)S(1)} fusion(bf16[80,8,128]{2,1,0:T(8,128)(2,1)} %bitcast.81, s32[1024]{0:T(1024)S(1)} %pad_clamp_fusion), kind=kCustom, calls=%fused_computation | custom fusion | bytes 24600 | tf_op jit(solution)/shard_map/gather | solution.py:321
  15.6 0.2 select_reduce_fusion.11
  16.0 0.1 and_reduce_fusion
  16.1 0.1 select_reduce_fusion.15
  16.2 0.6 reduce_max.9
  17.5 0.1 copy.95
  17.7 0.2 select_reduce_fusion.10
  17.9 0.2 select_reduce_fusion.12
  18.2 0.1 fusion.8
  18.4 6.3 %fusion.6 = bf16[6,64,8,128]{3,2,1,0:T(8,128)(2,1)S(1)} fusion(bf16[6,64,128,128]{3,2,1,0:T(8,128)(2,1)} %param.10, pred[6]{0:T(512)(128)(4,1)S(1)} %iota_compare_fusion.3, bf16[6,8,128]{2,1,0:T(8,128)(2,1)S(1)} %gather_fusion), kind=kOutput, calls=%fused_computation.44 | convolution fusion | flops 101449728 | bytes 13381638 | tf_op jit(solution)/shard_map/sim,spmn->spin/dot_general | solution.py:322
  24.7 106.7 %conditional.1 = (bf16[32,8,2304]{2,1,0:T(8,128)(2,1)S(1)}) conditional(s32[]{:T(128)} %convert_element_type.9, (s32[]{:T(128)}, s32[8]{0:T(128)S(1)}, s32[8,6]{1,0:T(8,128)S(1)}, s32[6]{0:T(128)S(1)}, s32[8,1,6]{2,0,1:T(8,128)S(1)}, /*index=5*/s32[6]{0:T(128)S(1)}, s32[1,3,6]{2,1,0:T(4,128)S(1)}, s32[8,3,6]{2,0,1:T(8,128)S(1)}, ...), branch_computations={%region_8.14_spmd.clone, %region_13.19_spmd.clone} | conditional | flops 8706 | bytes 17822 | solution.py:358
  24.9 0.1 select_reduce_fusion.8
  25.0 0.7 select_reduce_fusion.9.pick_ref
  25.8 0.1 and_bitcast_fusion.4
  25.9 0.1 select_reduce_fusion.7
  26.1 0.1 copy.87
  26.3 0.6 reshape.328.idx_ref
  26.9 0.3 select_reduce_fusion.6
  27.2 0.1 and_bitcast_fusion.3
  27.3 0.1 select_reduce_fusion.5
  27.4 0.1 copy.89
  27.5 0.7 reshape.329.w_ref
  28.3 103.2 %branch_1_fun.2 = bf16[256,2304]{1,0:T(8,128)(2,1)S(1)} custom-call(s32[24]{0:T(128)} %reshape.328.idx_ref, f32[240]{0:T(256)} %reshape.329.w_ref, s32[10]{0:T(128)} %select_reduce_fusion.9.pick_ref, bf16[6,2,256,128]{3,2,1,0:T(8,128)(2,1)S(1)} %bitcast.65, bf16[10,128,2304]{2,1,0:T(8,128)(2,1)} %bitcast.63), custom_call_target="tpu_custom_call" | custom-call | tf_op jit(solution)/shard_map/cond/branch_1_fun/pallas_call | solution.py:269
  131.4 1.0 copy.106
  (40 shorter events, 1.0 us)
where the time goes:
time: 133 us; the launch traced here: 132 us
  Pallas kernels  112 us (84%)
  local copies, waits for them, and re-layouts  7.93 us (6%)
  matrix products  6.31 us (5%)
  other arithmetic  4.35 us (3%)
  between operations  1.42 us (1%)
    pallas_call x1, Pallas kernels, fused(): pl.pallas_call(functools.partial(main_kernel, n, nz, kept), out_shape=jax...  103 us
    pallas_call x1, Pallas kernels, gather_small(): pl.pallas_call(functools.partial(small_kernel, n), out_shape=(jax.ShapeDt...  9.03 us
    dot_general x1, matrix products, per_device(): jnp.einsum('sim,spmn->spin', occ_pick, blocks, preferred_element_type=jnp...  6.31 us

commit v1 on v0

v1 whole, which is shorter than its diff:
```python
import functools

import jax
import jax.numpy as jnp
from jax import lax
from jax.experimental import pallas as pl
from jax.experimental.pallas import tpu as pltpu
from jax.sharding import PartitionSpec as P

MESH = pl.DeviceIdType.MESH
CAP = 3
CHUNKS = 4
TAB_ROWS = 32
f32 = jnp.float32
bf16 = jnp.bfloat16


def block_place(block_ids, owned_all):
    hits = block_ids[..., None] == owned_all
    positions = jnp.arange(owned_all.shape[0], dtype=jnp.int32)
    return jnp.sum(jnp.where(hits, positions, 0), axis=-1)


def iota2(shape, axis):
    return lax.broadcasted_iota(jnp.int32, shape, axis)


def make_tables(n, slots, per_owner, chip, variants, flat, tab_ref):
    total, owned, cap = n * slots, n * per_owner, 2 * slots
    chips, most, zero_slab = n // 2, n * CAP, n * slots
    flat = flat.astype(f32)
    nu_row, live_row, own_row = flat[1:2], flat[2:3] > 0, flat[3:4]
    o0, o1 = iota2((owned, 128), 0), iota2((owned, 128), 1)
    own_col = jnp.sum(jnp.where(o0 == o1, own_row, 0.0), axis=1, keepdims=True)
    place_mu, place = (
        jnp.sum(jnp.where(own_col == row, o0.astype(f32), 0.0), axis=0, keepdims=True) for row in (flat[0:1], nu_row)
    )
    t0, t1 = iota2((total, 128), 0), iota2((total, 128), 1)
    lane = t1.astype(f32)
    lane1 = lane[0:1]
    before = t0 < t1

    def steps(row, size, count):
        return sum(jnp.where(row >= float(size * q), 1.0, 0.0) for q in range(1, count))

    def col(row):
        return jnp.sum(jnp.where(t0 == t1, row, 0.0), axis=1, keepdims=True)

    def down(mask, value=1.0):
        return jnp.sum(jnp.where(mask, value, 0.0), axis=0, keepdims=True)

    dead = -1.0 - lane1
    to_chip = steps(place, 2 * per_owner, chips)
    from_chip = steps(lane1, cap, chips)
    key = jnp.where(live_row, place, dead)
    pair = jnp.where(live_row, from_chip * chips + to_chip, dead)
    dest = jnp.where(live_row, to_chip, dead)
    key_col, pair_col, dest_col, from_col = col(key), col(pair), col(dest), col(from_chip)
    same = key_col == key
    pos = down((pair_col == pair) & before)
    copies = down(same & before)
    first = jnp.where(live_row & (copies == 0.0), 1.0, 0.0)
    first_col = col(first) > 0
    order = down(first_col & (dest_col == dest) & before)
    rank = down(same & first_col, col(order))
    pos_col, copies_col, rank_col = col(pos), col(copies), col(rank)
    mine = dest_col == chip
    hit = mine & (rank_col == lane)
    loc = jnp.where(hit, from_col * cap + pos_col - zero_slab, 0.0)

    def put(row, value):
        tab_ref[row:row + 1, :] = value.astype(jnp.int32)

    for j in range(most):
        put(j, down(copies_col == float(j), loc) + zero_slab)
    put(most, down(hit & first_col, col(place) - 2 * per_owner * chip))
    slot_col = t0.astype(f32)[:, 0:1] - cap * chip
    for q in range(chips):
        put(most + 1 + q, down((from_col == chip) & (dest_col == float(q)) & (pos_col == lane), slot_col))

    def top(row):
        return jnp.max(jnp.where(live_row, row, 0.0), axis=1, keepdims=True)

    crossing = jnp.where(to_chip == from_chip, 0.0, pos + 1.0)
    sizes = (top(rank + 1.0), top(copies + 1.0), top(crossing))
    which = jnp.zeros((1, 1), f32)
    for limits in variants[:-1]:
        over = sum(jnp.where(size > float(limit), 1.0, 0.0) for size, limit in zip(sizes, limits))
        which = which + jnp.where(over > 0, 1.0, 0.0)
    put(most + 1 + chips, jnp.broadcast_to(which, (1, 128)))
    return place_mu


def prep_kernel(
    n, variants, pairs_hbm, counts_hbm, owned_hbm, occ_hbm, blk_hbm, tab_ref, all_ref,
    pairs_ref, counts_ref, owned_ref,
    blk, mscr, msnd, mall, occ_all, lhs, hsnd, b_sem, i_sem, m_s, m_r, o_s, o_r, h_s, h_r,
):
    me = lax.axis_index("ao")
    core = lax.rem(me, 2)
    mate = me + 1 - 2 * core
    slots, deep = blk.shape[0], blk.shape[1]
    per_owner = owned_ref.shape[1]
    rows = occ_hbm.shape[0]
    occupied = rows // per_owner
    barrier = pltpu.get_barrier_semaphore()
    for k in range(1, n):
        pl.semaphore_signal(barrier, inc=1, device_id={"ao": lax.rem(me + k, n)}, device_id_type=MESH)
    reads = [pltpu.make_async_copy(blk_hbm.at[s], blk.at[s], b_sem.at[s]) for s in range(slots)]
    own_occ = occ_all.at[me]
    inputs = [
        pltpu.make_async_copy(src, dst, i_sem.at[i]) for i, (src, dst) in enumerate((
            (pairs_hbm, pairs_ref), (counts_hbm, counts_ref), (owned_hbm, owned_ref), (occ_hbm, own_occ),
        ))
    ]
    for copy in inputs + reads:
        copy.start()
    for copy in inputs:
        copy.wait()
    mscr[...] = jnp.zeros(mscr.shape, jnp.int32)
    mscr[0:2, 0:slots] = pairs_ref[...]
    mscr[2:3, 0:slots] = jnp.where(iota2((1, slots), 1) < counts_ref[...], 1, 0)
    mscr[3:4, 0:per_owner] = owned_ref[...]
    meta = mscr[...]
    by_slot, by_owner = pltpu.roll(meta, me * slots, 1), pltpu.roll(meta, me * per_owner, 1)
    meta = jnp.where(iota2(meta.shape, 0) == 3, by_owner, by_slot)
    msnd[...] = meta
    mall[me] = meta
    with jax.named_scope("barrier"):
        pl.semaphore_wait(barrier, n - 1)
    sent = []
    for k in range(1, n):
        to = {"ao": lax.rem(me + k, n)}
        for src, dst, ss, rs in ((msnd, mall, m_s, m_r), (own_occ, occ_all, o_s, o_r)):
            copy = pltpu.make_async_remote_copy(
                src_ref=src, dst_ref=dst.at[me], send_sem=ss.at[k], recv_sem=rs.at[k],
                device_id=to, device_id_type=MESH,
            )
            copy.start()
            sent.append(copy)
    with jax.named_scope("meta_wait"):
        for copy in sent:
            copy.wait_recv()
    flat = mall[0]
    for r in range(1, n):
        flat = flat + mall[r]
    chip = (me // 2).astype(f32)
    with jax.named_scope("tables"):
        place_mu = make_tables(n, slots, per_owner, chip, variants, flat, tab_ref)

    pair_rows = 2 * occupied * slots
    r0, r1 = iota2((pair_rows, 128), 0), iota2((pair_rows, 128), 1)
    mine = r1 == me * slots + r0 // (2 * occupied)
    want = jnp.sum(jnp.where(mine, place_mu, 0.0), axis=1, keepdims=True) * occupied
    wide = (pair_rows, n * rows)
    want = want + (lax.rem(r0, occupied)).astype(f32)[:, 0:1]
    pick = jnp.where(iota2(wide, 1).astype(f32) == want, 1.0, 0.0).astype(bf16)
    occ = occ_all[...].reshape(n * rows, 128)
    picked = jnp.dot(pick, occ, preferred_element_type=f32)
    upper = lax.rem(r0 // occupied, 2) == 0
    lhs[:, 0:128] = jnp.where(upper, picked, 0.0).astype(bf16)
    lhs[:, 128:256] = jnp.where(upper, 0.0, picked).astype(bf16)

    group = 2 * occupied
    halves = deep // 4
    passed = []
    for s in range(slots):
        with jax.named_scope("read_wait"):
            reads[s].wait()
        left = lhs[s * group:(s + 1) * group, :]

        def product(q):
            right = blk[s, pl.ds(2 * q, 2)].reshape(256, 128)
            return jnp.dot(left, right, preferred_element_type=f32).astype(bf16)

        def out_rows(q):
            return pl.ds(pl.multiple_of(q * group, group), group)

        @pl.loop(0, halves, unroll=8)
        def _(q):
            hsnd[s, out_rows(q), :] = product((1 - core) * halves + q)

        copy = pltpu.make_async_remote_copy(
            src_ref=hsnd.at[s], dst_ref=all_ref.at[core * slots + s], send_sem=h_s.at[s], recv_sem=h_r.at[s],
            device_id={"ao": mate}, device_id_type=MESH,
        )
        copy.start()
        passed.append(copy)

        @pl.loop(0, halves, unroll=8)
        def _(q):
            all_ref[core * slots + s, out_rows(q), :] = product(core * halves + q)

    with jax.named_scope("end_wait"):
        for copy in passed:
            copy.wait()
    for copy in sent:
        copy.wait_send()


def prepare(n, variants, pairs, counts, owned, occ, blocks):
    slots, deep, _, width = blocks.shape
    per_owner, occupied, _ = occ.shape
    rows = per_owner * occupied
    span = deep * occupied // 2
    dma, vm = pltpu.SemaphoreType.DMA, pltpu.VMEM
    whole = pl.BlockSpec(memory_space=pltpu.VMEM)
    return pl.pallas_call(
        functools.partial(prep_kernel, n, variants),
        out_shape=(
            jax.ShapeDtypeStruct((TAB_ROWS, 128), jnp.int32),
            jax.ShapeDtypeStruct((2 * slots, span, width), bf16),
        ),
        in_specs=[pl.BlockSpec(memory_space=pl.ANY)] * 5,
        out_specs=(whole, whole),
        scratch_shapes=[
            vm((2, slots), jnp.int32), vm((1, 1), jnp.int32), vm((1, per_owner), jnp.int32),
            vm(blocks.shape, bf16),
            vm((8, 128), jnp.int32), vm((8, 128), jnp.int32), vm((n, 8, 128), jnp.int32),
            vm((n, rows, width), bf16),
            vm((2 * occupied * slots, 2 * width), bf16),
            vm((slots, span, width), bf16),
            dma((slots,)), dma((4,)), dma((n,)), dma((n,)), dma((n,)), dma((n,)), dma((slots,)), dma((slots,)),
        ],
        compiler_params=pltpu.CompilerParams(
            collective_id=0, has_side_effects=True, vmem_limit_bytes=62 * 1024 * 1024,
        ),
    )(pairs.T, counts.reshape(1, 1), owned.reshape(1, per_owner), occ.reshape(rows, width), blocks)


def main_kernel(n, nz, kept, depth_j, cross, tab_ref, all_ref, vir_hbm, out_ref, *refs):
    (vir_both, vir, snd, rows, part, rx, ry, tx, ty, vir_sem, vir_s, vir_r, a_s, a_r,
     up_s, up_r, dn_s, dn_r, x_s, x_r, y_s, y_r) = refs[:22]
    rcv = refs[22:]
    me, z = lax.axis_index("ao"), lax.axis_index("aux")
    core, chip = lax.rem(me, 2), me // 2
    cx, cy = lax.rem(chip, 2), chip // 2
    mate = me + 1 - 2 * core
    xmate = me + 2 - 4 * cx
    ymate = me + 4 - 8 * cy
    dmate = xmate + 4 - 8 * cy
    others = (xmate, ymate, dmate)
    cap, span, width = all_ref.shape
    per_owner = vir_hbm.shape[0]
    most = n * CAP
    zero_slab = n // 2 * cap
    step = span // CHUNKS
    mid = step // 2

    barrier = pltpu.get_barrier_semaphore()
    for to in (mate,) + others:
        pl.semaphore_signal(barrier, inc=1, device_id={"ao": to}, device_id_type=MESH)
    for k in range(1, nz):
        pl.semaphore_signal(barrier, inc=1, device_id={"aux": lax.rem(z + k, nz)}, device_id_type=MESH)
    own_vir = vir_both.at[pl.ds(core * per_owner, per_owner)]
    vir_copy = pltpu.make_async_copy(vir_hbm, own_vir, vir_sem)
    vir_copy.start()

    with jax.named_scope("pack"):
      for d, to in enumerate(others):
        for j in range(cross):
            snd[d, j] = all_ref[tab_ref[most + 1 + to // 2, j]]
    for j in range(cap):
        slab = all_ref[tab_ref[most + 1 + chip, j]]
        for c in range(CHUNKS):
            rcv[c][chip * cap + j] = slab[c * step:(c + 1) * step]
    for c in range(CHUNKS):
        rcv[c][zero_slab] = jnp.zeros((step, width), bf16)
    with jax.named_scope("barrier2"):
        pl.semaphore_wait(barrier, 1 + len(others) + nz - 1)

    def remote(src, dst, ss, rs, to):
        copy = pltpu.make_async_remote_copy(
            src_ref=src, dst_ref=dst, send_sem=ss, recv_sem=rs, device_id={"ao": to}, device_id_type=MESH,
        )
        copy.start()
        return copy

    a_copies = []
    for c in range(CHUNKS):
        at = pl.ds(chip * cap, cross)
        a_copies.append([
            remote(snd.at[d, :, pl.ds(c * step, step), :], rcv[c].at[at], a_s.at[c, d], a_r.at[c, d], to)
            for d, to in enumerate(others)
        ])
    with jax.named_scope("vir_wait"):
        vir_copy.wait()
    vir_pass = remote(own_vir, own_vir, vir_s, vir_r, mate)

    def z_copy(c, d, up):
        src = z - d if up else z + d
        return pltpu.make_async_remote_copy(
            src_ref=rows.at[c, src], dst_ref=rows.at[c, src],
            send_sem=(up_s if up else dn_s).at[c, d], recv_sem=(up_r if up else dn_r).at[c, d],
            device_id={"aux": z + 1 if up else z - 1}, device_id_type=MESH,
        )

    def z_send(c, d):
        @pl.when((z - d >= 0) & (z + 1 < nz))
        def _():
            z_copy(c, d, True).start()

        @pl.when((z + d < nz) & (z >= 1))
        def _():
            z_copy(c, d, False).start()

    def z_recv(c, d, up):
        src = z - d if up else z + d
        return pltpu.make_async_remote_copy(
            src_ref=rows.at[c, src], dst_ref=rows.at[c, src],
            send_sem=(up_s if up else dn_s).at[c, d - 1], recv_sem=(up_r if up else dn_r).at[c, d - 1],
            device_id={"aux": z - 1 if up else z + 1}, device_id_type=MESH,
        )

    def stage_a(c):
        for copy in a_copies[c]:
            copy.wait_recv()

        @pl.loop(0, kept)
        def _(k):
            acc = rcv[c][tab_ref[0, k]].astype(f32)
            for j in range(1, depth_j):
                acc = acc + rcv[c][tab_ref[j, k]].astype(f32)
            rows[c, z, :, pl.ds(pl.multiple_of(k * width, width), width)] = acc.astype(bf16)

        z_send(c, 0)

    def stage_b(c, d):
        @pl.when(z - d >= 0)
        def _():
            z_recv(c, d, True).wait_recv()

        @pl.when(z + d < nz)
        def _():
            z_recv(c, d, False).wait_recv()

        if d < nz - 1:
            z_send(c, d)

    x_copies, y_copies = {}, {}
    tile = 256
    depth = rows.shape[-1]
    piece = 16

    def stage_v():
        vir_pass.wait_recv()

        @pl.loop(0, width // piece)
        def _(i):
            at = pl.ds(pl.multiple_of(i * piece, piece), piece)
            for k in range(kept):
                to = pl.ds(pl.multiple_of(k * width + i * piece, piece), piece)
                vir[to, :] = vir_both[tab_ref[most, k], at, :]

    lo, hi = pl.ds(0, mid), pl.ds(mid, mid)

    def stage_m(c):
        @pl.loop(0, vir.shape[1] // tile)
        def _(j):
            cols = pl.ds(pl.multiple_of(j * tile, tile), tile)
            left = rows[c].reshape(nz * step, depth)
            got = jnp.dot(left, vir[:, cols], preferred_element_type=f32)
            part[c, :, :, cols] = got.astype(bf16).reshape(nz, step, tile)

        far = 2 * (1 - cy) + 1 - cx
        x_copies[c] = [
            remote(part.at[c, far, lo], rx.at[c, 0], x_s.at[c, 0], x_r.at[c, 0], xmate),
            remote(part.at[c, far, hi], ry.at[c, 0], y_s.at[c, 0], y_r.at[c, 0], ymate),
            remote(part.at[c, 2 * cy + 1 - cx, lo], rx.at[c, 1], x_s.at[c, 1], x_r.at[c, 1], xmate),
            remote(part.at[c, 2 * (1 - cy) + cx, hi], ry.at[c, 1], y_s.at[c, 1], y_r.at[c, 1], ymate),
        ]

    def add2(a, b):
        return (a.astype(f32) + b.astype(f32)).astype(bf16)

    def stage_x(c):
        for copy in x_copies[c][:2]:
            copy.wait_recv()
        tx[c] = add2(part[c, 2 * (1 - cy) + cx, :mid], rx[c, 0])
        ty[c] = add2(part[c, 2 * cy + 1 - cx, mid:], ry[c, 0])
        y_copies[c] = [
            remote(tx.at[c], rx.at[c, 2], y_s.at[c, 2], y_r.at[c, 2], ymate),
            remote(ty.at[c], ry.at[c, 2], x_s.at[c, 2], x_r.at[c, 2], xmate),
        ]

    def stage_y(c):
        for copy in x_copies[c][2:] + y_copies[c]:
            copy.wait_recv()
        own = part[c, chip]
        top = own[:mid].astype(f32) + rx[c, 1].astype(f32) + rx[c, 2].astype(f32)
        low = own[mid:].astype(f32) + ry[c, 1].astype(f32) + ry[c, 2].astype(f32)
        out_ref[c * step:c * step + mid, :] = top.astype(bf16)
        out_ref[c * step + mid:(c + 1) * step, :] = low.astype(bf16)

    plan = (
        "A0 A1 B01 B02", "A2 V B03 M0", "B11 B12 A3 X0", "B13 M1 B21 B22", "X1 Y0 B23 M2",
        "B31 B32 X2 Y1", "B33 M3 X3", "Y2 Y3",
    )
    run = {"A": stage_a, "B": stage_b, "M": stage_m, "X": stage_x, "Y": stage_y, "V": stage_v}
    for item in [name for row in plan for name in row.split()]:
        with jax.named_scope(item):
            run[item[0]](*[int(v) for v in item[1:]])

    vir_pass.wait_send()
    for c in range(CHUNKS):
        for copy in a_copies[c] + x_copies[c] + y_copies[c]:
            copy.wait_send()
        for d in range(nz - 1):
            @pl.when((z - d >= 0) & (z + 1 < nz))
            def _():
                z_copy(c, d, True).wait_send()

            @pl.when((z + d < nz) & (z >= 1))
            def _():
                z_copy(c, d, False).wait_send()


def fused(n, nz, sizes, call_id, tab, slabs, vir3):
    kept, depth_j, cross = sizes
    cap, span, width = slabs.shape
    per_owner, _, columns = vir3.shape
    step = span // CHUNKS
    dma, vm = pltpu.SemaphoreType.DMA, pltpu.VMEM
    return pl.pallas_call(
        functools.partial(main_kernel, n, nz, kept, depth_j, cross),
        out_shape=jax.ShapeDtypeStruct((span, columns), bf16),
        in_specs=[
            pl.BlockSpec(memory_space=pltpu.SMEM),
            pl.BlockSpec(memory_space=pltpu.VMEM),
            pl.BlockSpec(memory_space=pl.ANY),
        ],
        out_specs=pl.BlockSpec(memory_space=pltpu.VMEM),
        scratch_shapes=[
            vm((2 * per_owner, width, columns), bf16),
            vm((kept * width, columns), bf16),
            vm((3, cross, span, width), bf16),
            vm((CHUNKS, nz, step, kept * width), bf16),
            vm((CHUNKS, nz, step, columns), bf16),
            vm((CHUNKS, 3, step // 2, columns), bf16),
            vm((CHUNKS, 3, step // 2, columns), bf16),
            vm((CHUNKS, step // 2, columns), bf16),
            vm((CHUNKS, step // 2, columns), bf16),
            dma, dma, dma,
            dma((CHUNKS, 3)), dma((CHUNKS, 3)),
            dma((CHUNKS, nz)), dma((CHUNKS, nz)), dma((CHUNKS, nz)), dma((CHUNKS, nz)),
            dma((CHUNKS, 3)), dma((CHUNKS, 3)), dma((CHUNKS, 3)), dma((CHUNKS, 3)),
        ] + [vm((n // 2 * cap + 1, step, width), bf16)] * CHUNKS,
        compiler_params=pltpu.CompilerParams(
            collective_id=call_id, has_side_effects=True, vmem_limit_bytes=62 * 1024 * 1024,
        ),
    )(tab, slabs, vir3)


def per_device(blocks, pairs, counts, owned_blocks, occ_coef, vir_coef):
    groups, nz = lax.axis_size("ao"), lax.axis_size("aux")
    slots, _, _, width = blocks.shape
    per_owner, occupied, _ = occ_coef.shape
    variants = ((10, 4, 6), (12, 6, 9), (2 * per_owner, groups * CAP, 2 * slots))
    tab, slabs = prepare(groups, variants, pairs, counts, owned_blocks, occ_coef, blocks)
    vir3 = vir_coef.reshape(per_owner, width, vir_coef.shape[1])
    which = tab[groups * CAP + 1 + groups // 2, 0]
    out = lax.switch(
        which, [functools.partial(fused, groups, nz, v, 1 + i) for i, v in enumerate(variants)], tab, slabs, vir3,
    )
    return out.reshape(-1, occupied, vir_coef.shape[1])


def per_device_general(blocks, pairs, counts, owned_blocks, occ_coef, vir_coef):
    groups = lax.axis_size("ao")
    own_index = lax.axis_index("ao")
    slot_count = blocks.shape[0]
    aux_depth = blocks.shape[1]
    block_width = blocks.shape[3]
    occupied = occ_coef.shape[1]
    all_pairs, all_counts, all_owned = (
        lax.all_gather(pairs, "ao", axis=0, tiled=True),
        lax.all_gather(counts, "ao", axis=0, tiled=True),
        lax.all_gather(owned_blocks, "ao", axis=0, tiled=True),
    )
    occ_all = lax.all_gather(occ_coef, "ao", axis=0, tiled=True)
    per_owner = all_owned.shape[0] // groups
    slot_ids = jnp.arange(slot_count, dtype=jnp.int32)
    in_use = slot_ids < counts[0]
    occ_pick = occ_all[block_place(pairs[:, 0], all_owned)]
    slab_values = jnp.einsum("sim,spmn->spin", occ_pick, blocks, preferred_element_type=jnp.float32)
    slab_values = jnp.where(in_use[:, None, None, None], slab_values, 0.0).astype(jnp.bfloat16)
    flat_slabs = slab_values.reshape(slot_count, aux_depth * occupied, block_width)
    place_all = block_place(all_pairs[:, 1], all_owned).reshape(groups, slot_count)
    owner_all = place_all // per_owner
    local_all = place_all % per_owner
    live_all = slot_ids[None, :] < all_counts[:, None]
    mine_all = live_all & (owner_all == own_index)
    local_ids = jnp.arange(per_owner, dtype=jnp.int32)
    slabs_got = lax.all_gather(flat_slabs, "ao", axis=0, tiled=True)
    assign = (
        mine_all.reshape(-1)[None, :] & (local_all.reshape(-1)[None, :] == local_ids[:, None])
    ).astype(jnp.bfloat16)
    summed = jnp.einsum("lt,tqm->qlm", assign, slabs_got, preferred_element_type=jnp.float32)
    rows_local = summed.reshape(summed.shape[0], per_owner * block_width).astype(jnp.bfloat16)
    rows_whole = lax.all_gather(rows_local, "aux", axis=0, tiled=True)
    share = rows_whole.shape[0] // groups
    result = lax.psum_scatter(
        jnp.dot(rows_whole, vir_coef, preferred_element_type=jnp.float32).astype(jnp.bfloat16),
        "ao",
        scatter_dimension=0,
        tiled=True,
    )
    return result.reshape(share // occupied, occupied, vir_coef.shape[1])


def solution(mesh):
    in_specs = (
        P("ao", "aux", None, None),
        P("ao", None),
        P("ao"),
        P("ao"),
        P("ao", None, None),
        P("ao", "aux"),
    )
    out_specs = P("ao", None, "aux")
    small = mesh.shape["ao"] == 8 and mesh.shape["aux"] == 4
    body = per_device if small else per_device_general
    return jax.shard_map(body, mesh=mesh, in_specs=in_specs, out_specs=out_specs, check_vma=False)
```

time: 133 us -> 92.8 us (0.70)
  Pallas kernels: 112 us -> 89.8 us
  local copies, waits for them, and re-layouts: 7.93 us -> 1.53 us
  matrix products: 6.31 us -> 0 us
  other arithmetic: 4.35 us -> 0 us
    pallas_call x2, Pallas kernels: 112 us -> 89.8 us  [the longest x1 73.6 us: fused(): pl.pallas_call(functools.partial(main_kernel, n, nz, kept, depth_j, cross...]
    dot_general x1 -> x0, matrix products: 6.31 us -> none  [per_device(): jnp.einsum('sim,spmn->spin', occ_pick, blocks, preferred_element_type=jnp...]
    reduce_sum x9 -> x0, other arithmetic: 2.09 us -> none  [the longest x1 0.66 us: per_device(): pick = jnp.sum(jnp.where(listed, positions[None, :], 0), axis=1)]
    gather x1 -> x0, local copies, waits for them, and re-layouts: 1.48 us -> none  [per_device(): occ_pick = occ_all[block_place(pairs[:, 0], all_owned)]]
    reshape x4 -> x0, local copies, waits for them, and re-layouts: 1.41 us -> none  [the longest x1 0.72 us: per_device(): weights = jnp.sum(jnp.where(weights, 1.0, 0.0), axis=-1).reshape(-1)]
where the time goes in v1:
time: 92.8 us; the launch traced here: 92.6 us
  Pallas kernels  89.8 us (97%)
  local copies, waits for them, and re-layouts  1.53 us (2%)
  between operations  1.32 us (1%)
    pallas_call x1, Pallas kernels, fused(): pl.pallas_call(functools.partial(main_kernel, n, nz, kept, depth_j, cross...  73.6 us
    pallas_call x1, Pallas kernels, prepare(): pl.pallas_call(functools.partial(prep_kernel, n, variants), out_shape=(ja...  16.1 us

profile of v1, /device:TPU:0, one launch (start us, length us, event | category | flops | bytes accessed | tf_op | source)
XLA Modules:
  0.0 92.6 jit_solution(12751475349129013982)
XLA Ops:
  0.7 16.1 %shard_map.67 = (s32[32,128]{1,0:T(8,128)S(1)}, bf16[12,256,128]{2,1,0:T(8,128)(2,1)S(1)}) custom-call(s32[2,6]{1,0:T(2,128)} %bitcast.17, s32[1,1]{1,0:T(1,128)} %bitcast.9.counts_hbm, s32[1,10]{1,0:T(1,128)} %bitcast.18, bf16[80,128]{1,0:T(8,128)(2,1)} %bitcast.16, bf16[6,64,128,128]{3,2,1,0:T(8,128)(2,1)} %blk_hbm.1), custom_call_target="tpu_custom_call" | custom-call | tf_op jit(solution)/shard_map/pallas_call | solution.py:208
  16.8 0.5 slice.3
  18.0 73.7 %conditional.1 = (bf16[32,8,2304]{2,1,0:T(8,128)(2,1)S(1)}) conditional(s32[]{:T(128)} %bitcast.7, (s32[32,128]{1,0:T(8,128)S(1)}, bf16[12,256,128]{2,1,0:T(8,128)(2,1)S(1)}, bf16[10,128,2304]{2,1,0:T(8,128)(2,1)}) %tuple.24, (s32[32,128]{1,0:T(8,128)S(1)}, bf16[12,256,128]{2,1,0:T(8,128)(2,1)S(1)}, ...), branch_computations={%region_0.0_spmd, %region_1.0_spmd, %region_2.0_spmd} | conditional | bytes 8 | solution.py:462
  18.0 73.6 %branch_0_fun.1 = bf16[256,2304]{1,0:T(8,128)(2,1)S(1)} custom-call(s32[32,128]{1,0:T(8,128)S(1)} %get-tuple-element.28.tab_ref, bf16[12,256,128]{2,1,0:T(8,128)(2,1)S(1)} %get-tuple-element.29.all_ref, bf16[10,128,2304]{2,1,0:T(8,128)(2,1)} %get-tuple-element.30.vir_hbm), custom_call_target="tpu_custom_call" | custom-call | tf_op jit(solution)/shard_map/cond/branch_0_fun/pallas_call | solution.py:424
  91.6 1.0 %copy.15 = bf16[32,8,2304]{2,1,0:T(8,128)(2,1)} copy(bf16[32,8,2304]{2,1,0:T(8,128)(2,1)S(1)} %get-tuple-element.41) | data formatting | bytes 2359296

commit v2 on v1

v2 whole, which is shorter than its diff:
```python
import functools

import jax
import jax.numpy as jnp
from jax import lax
from jax.experimental import pallas as pl
from jax.experimental.pallas import tpu as pltpu
from jax.sharding import PartitionSpec as P

MESH = pl.DeviceIdType.MESH
CAP = 3
CHUNKS = (1,) * 8
VARIANTS = ((8, 4, 6), (10, 4, 6), (10, 4, 9), (12, 6, 9))
TAB_ROWS = 32
f32 = jnp.float32
bf16 = jnp.bfloat16


def block_place(block_ids, owned_all):
    hits = block_ids[..., None] == owned_all
    positions = jnp.arange(owned_all.shape[0], dtype=jnp.int32)
    return jnp.sum(jnp.where(hits, positions, 0), axis=-1)


def iota2(shape, axis):
    return lax.broadcasted_iota(jnp.int32, shape, axis)


def make_tables(n, slots, per_owner, chip, variants, flat, tab_ref, which_ref):
    total, owned, cap = n * slots, n * per_owner, 2 * slots
    chips, most, zero_slab = n // 2, n * CAP, n * slots
    flat = flat.astype(f32)
    nu_row, live_row, own_row = flat[1:2], flat[2:3] > 0, flat[3:4]
    o0, o1 = iota2((owned, 128), 0), iota2((owned, 128), 1)
    own_col = jnp.sum(jnp.where(o0 == o1, own_row, 0.0), axis=1, keepdims=True)
    place_mu, place = (
        jnp.sum(jnp.where(own_col == row, o0.astype(f32), 0.0), axis=0, keepdims=True) for row in (flat[0:1], nu_row)
    )
    t0, t1 = iota2((total, 128), 0), iota2((total, 128), 1)
    lane = t1.astype(f32)
    lane1 = lane[0:1]
    before = t0 < t1

    def steps(row, size, count):
        return sum(jnp.where(row >= float(size * q), 1.0, 0.0) for q in range(1, count))

    def col(row):
        return jnp.sum(jnp.where(t0 == t1, row, 0.0), axis=1, keepdims=True)

    def down(mask, value=1.0):
        return jnp.sum(jnp.where(mask, value, 0.0), axis=0, keepdims=True)

    dead = -1.0 - lane1
    to_chip = steps(place, 2 * per_owner, chips)
    from_chip = steps(lane1, cap, chips)
    key = jnp.where(live_row, place, dead)
    pair = jnp.where(live_row, from_chip * chips + to_chip, dead)
    dest = jnp.where(live_row, to_chip, dead)
    key_col, pair_col, dest_col, from_col = col(key), col(pair), col(dest), col(from_chip)
    same = key_col == key
    pos = down((pair_col == pair) & before)
    copies = down(same & before)
    first = jnp.where(live_row & (copies == 0.0), 1.0, 0.0)
    first_col = col(first) > 0
    order = down(first_col & (dest_col == dest) & before)
    rank = down(same & first_col, col(order))
    pos_col, copies_col, rank_col = col(pos), col(copies), col(rank)
    mine = dest_col == chip
    hit = mine & (rank_col == lane)
    loc = jnp.where(hit, from_col * cap + pos_col - zero_slab, 0.0)

    def put(row, value):
        tab_ref[row:row + 1, :] = value.astype(jnp.int32)

    for j in range(most):
        put(j, down(copies_col == float(j), loc) + zero_slab)
    put(most, down(hit & first_col, col(place) - 2 * per_owner * chip))
    slot_col = t0.astype(f32)[:, 0:1] - cap * chip
    for q in range(chips):
        put(most + 1 + q, down((from_col == chip) & (dest_col == float(q)) & (pos_col == lane), slot_col))

    def top(row):
        return jnp.max(jnp.where(live_row, row, 0.0), axis=1, keepdims=True)

    crossing = jnp.where(to_chip == from_chip, 0.0, pos + 1.0)
    sizes = (top(rank + 1.0), top(copies + 1.0), top(crossing))
    which = jnp.zeros((1, 1), f32)
    for limits in variants[:-1]:
        over = sum(jnp.where(size > float(limit), 1.0, 0.0) for size, limit in zip(sizes, limits))
        which = which + jnp.where(over > 0, 1.0, 0.0)
    which_ref[...] = which.astype(jnp.int32)
    return place_mu


def prep_kernel(
    n, variants, pairs_hbm, counts_hbm, owned_hbm, occ_hbm, tab_ref, lhs, which_ref,
    pairs_ref, counts_ref, owned_ref, mscr, msnd, mall, occ_all, i_sem, m_s, m_r, o_s, o_r,
):
    me = lax.axis_index("ao")
    slots = pairs_ref.shape[1]
    per_owner = owned_ref.shape[1]
    rows = occ_hbm.shape[0]
    occupied = rows // per_owner
    barrier = pltpu.get_barrier_semaphore()
    for k in range(1, n):
        pl.semaphore_signal(barrier, inc=1, device_id={"ao": lax.rem(me + k, n)}, device_id_type=MESH)
    own_occ = occ_all.at[me]
    inputs = [
        pltpu.make_async_copy(src, dst, i_sem.at[i]) for i, (src, dst) in enumerate((
            (pairs_hbm, pairs_ref), (counts_hbm, counts_ref), (owned_hbm, owned_ref), (occ_hbm, own_occ),
        ))
    ]
    for copy in inputs:
        copy.start()
    for copy in inputs:
        copy.wait()
    mscr[...] = jnp.zeros(mscr.shape, jnp.int32)
    mscr[0:2, 0:slots] = pairs_ref[...]
    mscr[2:3, 0:slots] = jnp.where(iota2((1, slots), 1) < counts_ref[...], 1, 0)
    mscr[3:4, 0:per_owner] = owned_ref[...]
    meta = mscr[...]
    by_slot, by_owner = pltpu.roll(meta, me * slots, 1), pltpu.roll(meta, me * per_owner, 1)
    meta = jnp.where(iota2(meta.shape, 0) == 3, by_owner, by_slot)
    msnd[...] = meta
    mall[me] = meta
    with jax.named_scope("barrier"):
        pl.semaphore_wait(barrier, n - 1)
    sent = []
    for k in range(1, n):
        to = {"ao": lax.rem(me + k, n)}
        for src, dst, ss, rs in ((msnd, mall, m_s, m_r), (own_occ, occ_all, o_s, o_r)):
            copy = pltpu.make_async_remote_copy(
                src_ref=src, dst_ref=dst.at[me], send_sem=ss.at[k], recv_sem=rs.at[k],
                device_id=to, device_id_type=MESH,
            )
            copy.start()
            sent.append(copy)
    with jax.named_scope("meta_wait"):
        for copy in sent:
            copy.wait_recv()
    flat = mall[0]
    for r in range(1, n):
        flat = flat + mall[r]
    chip = (me // 2).astype(f32)
    with jax.named_scope("tables"):
        place_mu = make_tables(n, slots, per_owner, chip, variants, flat, tab_ref, which_ref)

    pair_rows = 2 * occupied * slots
    r0, r1 = iota2((pair_rows, 128), 0), iota2((pair_rows, 128), 1)
    mine = r1 == me * slots + r0 // (2 * occupied)
    want = jnp.sum(jnp.where(mine, place_mu, 0.0), axis=1, keepdims=True) * occupied
    wide = (pair_rows, n * rows)
    want = want + (lax.rem(r0, occupied)).astype(f32)[:, 0:1]
    pick = jnp.where(iota2(wide, 1).astype(f32) == want, 1.0, 0.0).astype(bf16)
    occ = occ_all[...].reshape(n * rows, 128)
    picked = jnp.dot(pick, occ, preferred_element_type=f32)
    upper = lax.rem(r0 // occupied, 2) == 0
    lhs[:, 0:128] = jnp.where(upper, picked, 0.0).astype(bf16)
    lhs[:, 128:256] = jnp.where(upper, 0.0, picked).astype(bf16)

    for copy in sent:
        copy.wait_send()


def prepare(n, variants, pairs, counts, owned, occ):
    slots = pairs.shape[0]
    per_owner, occupied, width = occ.shape
    rows = per_owner * occupied
    dma, vm = pltpu.SemaphoreType.DMA, pltpu.VMEM
    whole = pl.BlockSpec(memory_space=pltpu.VMEM)
    return pl.pallas_call(
        functools.partial(prep_kernel, n, variants),
        out_shape=(
            jax.ShapeDtypeStruct((TAB_ROWS, 128), jnp.int32),
            jax.ShapeDtypeStruct((2 * occupied * slots, 2 * width), bf16),
            jax.ShapeDtypeStruct((1, 1), jnp.int32),
        ),
        in_specs=[pl.BlockSpec(memory_space=pl.ANY)] * 4,
        out_specs=(whole,) * 3,
        scratch_shapes=[
            vm((2, slots), jnp.int32), vm((1, 1), jnp.int32), vm((1, per_owner), jnp.int32),
            vm((8, 128), jnp.int32), vm((8, 128), jnp.int32), vm((n, 8, 128), jnp.int32),
            vm((n, rows, width), bf16),
            dma((4,)), dma((n,)), dma((n,)), dma((n,)), dma((n,)),
        ],
        compiler_params=pltpu.CompilerParams(
            collective_id=0, has_side_effects=True, vmem_limit_bytes=62 * 1024 * 1024,
        ),
    )(pairs.T, counts.reshape(1, 1), owned.reshape(1, per_owner), occ.reshape(rows, width))


def cuts(span):
    out, at = [], 0
    for part in CHUNKS:
        out.append((at, part * span // 8))
        at += part * span // 8
    return out


def make_plan(count):
    out = ["H0"]
    for c in range(1, count + 1):
        out += ["H%d" % c] + ["W"] * (c == count - 1) + ["P%d" % (c - 1)]
    out += ["A0", "A1", "F0", "A2", "F1", "V", "A3", "F2", "M0"]
    for c in range(count):
        out += ["A%d" % (c + 4), "F%d" % (c + 3), "M%d" % (c + 1), "X%d" % c, "Y%d" % (c - 1)]
        out += ["S%d" % (c - 2), "T%d" % (c - 3)]
    out += ["Y%d" % (count - 1)]
    out += ["S%d" % c for c in range(count - 2, count)] + ["T%d" % c for c in range(count - 3, count)]
    return [name for name in out if len(name) == 1 or 0 <= int(name[1:]) < count]


def main_kernel(n, nz, kept, depth_j, cross, tab_ref, lhs_ref, blk_hbm, vir_hbm, out_hbm, out_ref, out_sem, *refs):
    (vir_both, vir, blk, hsnd, snd, rows, part, rx, ry, tx, ty, vir_sem, vir_s, vir_r, b_sem, h_s, h_r, a_s, a_r,
     up_s, up_r, dn_s, dn_r, x_s, x_r, y_s, y_r) = refs[:27]
    pieces = refs[27:]
    count = len(pieces) // 2
    slab, rcv = pieces[:count], pieces[count:]
    me, z = lax.axis_index("ao"), lax.axis_index("aux")
    core, chip = lax.rem(me, 2), me // 2
    cx, cy = lax.rem(chip, 2), chip // 2
    mate = me + 1 - 2 * core
    xmate = me + 2 - 4 * cx
    ymate = me + 4 - 8 * cy
    others = (xmate, ymate, xmate + 4 - 8 * cy)
    slots, span, width = hsnd.shape
    cap = 2 * slots
    deep = blk.shape[1] // 2
    occupied = span // deep
    group = 2 * occupied
    per_owner = vir_hbm.shape[0]
    most = n * CAP
    zero_slab = n // 2 * cap
    chunks = cuts(span)

    barrier = pltpu.get_barrier_semaphore()
    for to in (mate,) + others:
        pl.semaphore_signal(barrier, inc=1, device_id={"ao": to}, device_id_type=MESH)

    for d in (1, 2):
        @pl.when(z + d < nz)
        def _():
            pl.semaphore_signal(barrier, inc=1, device_id={"aux": z + d}, device_id_type=MESH)

        @pl.when(z - d >= 0)
        def _():
            pl.semaphore_signal(barrier, inc=1, device_id={"aux": z - d}, device_id_type=MESH)

    reads = []
    for c, (at, step) in enumerate(chunks):
        pair = []
        for i, half in enumerate((1 - core, core)):
            these = pl.ds(half * deep + at // occupied, step // occupied)
            pair.append(pltpu.make_async_copy(blk_hbm.at[:, these], blk.at[:, these], b_sem.at[c, i]))
            pair[-1].start()
        reads.append(pair)
    own_vir = vir_both.at[pl.ds(core * per_owner, per_owner)]
    vir_copy = pltpu.make_async_copy(vir_hbm, own_vir, vir_sem)
    vir_copy.start()

    def remote(src, dst, ss, rs, to):
        copy = pltpu.make_async_remote_copy(
            src_ref=src, dst_ref=dst, send_sem=ss, recv_sem=rs, device_id={"ao": to}, device_id_type=MESH,
        )
        copy.start()
        return copy

    h_copies, a_copies, vir_pass = {}, {}, []

    def stage_h(c):
        at, step = chunks[c]

        def product(s, half, q):
            right = blk[s, pl.ds(half * deep + at // occupied + 2 * q, 2)].reshape(2 * width, width)
            left = lhs_ref[pl.ds(pl.multiple_of(s * group, group), group), :]
            return jnp.dot(left, right, preferred_element_type=f32).astype(bf16)

        for copy in reads[c]:
            copy.wait()

        @pl.loop(0, slots, unroll=3)
        def _(s):
            for q in range(step // group):
                hsnd[s, at + q * group:at + (q + 1) * group, :] = product(s, 1 - core, q)
                slab[c][core * slots + s, q * group:(q + 1) * group, :] = product(s, core, q)

        if c == 0:
            for w in range(2):
                @pl.when((z >= 1) & (z + 1 < nz) if w else (z < 1) | (z + 1 >= nz))
                def _():
                    pl.semaphore_wait(barrier, 6 + w)
        h_copies[c] = remote(
            hsnd.at[:, pl.ds(at, step), :], slab[c].at[pl.ds(core * slots, slots)], h_s.at[c], h_r.at[c], mate,
        )

    def stage_p(c):
        at, step = chunks[c]
        h_copies[c].wait_recv()
        for d, to in enumerate(others):
            for j in range(cross):
                snd[d, j, at:at + step, :] = slab[c][tab_ref[most + 1 + to // 2, j]]
        a_copies[c] = [
            remote(snd.at[d, :, pl.ds(at, step), :], rcv[c].at[pl.ds(chip * cap, cross)], a_s.at[c, d], a_r.at[c, d], to)
            for d, to in enumerate(others)
        ]
        for j in range(cap):
            rcv[c][chip * cap + j] = slab[c][tab_ref[most + 1 + chip, j]]
        rcv[c][zero_slab] = jnp.zeros((step, width), bf16)

    def stage_w():
        vir_copy.wait()
        vir_pass.append(remote(own_vir, own_vir, vir_s, vir_r, mate))

    def z_copy(c, d, up):
        src = z if d < 3 else z - 2 if up else z + 2
        hop = min(d, 2) if d < 3 else 1
        return pltpu.make_async_remote_copy(
            src_ref=rows.at[src, pl.ds(*chunks[c])], dst_ref=rows.at[src, pl.ds(*chunks[c])],
            send_sem=(up_s if up else dn_s).at[c, d], recv_sem=(up_r if up else dn_r).at[c, d],
            device_id={"aux": z + hop if up else z - hop}, device_id_type=MESH,
        )

    def z_sends(d, up):
        if d < 3:
            return z + d < nz if up else z - d >= 0
        return (z >= 2) & (z + 1 < nz) if up else (z + 2 < nz) & (z >= 1)

    def z_recv(c, d, up):
        src = z - d if up else z + d
        hop = d if d < 3 else 1
        return pltpu.make_async_remote_copy(
            src_ref=rows.at[src, pl.ds(*chunks[c])], dst_ref=rows.at[src, pl.ds(*chunks[c])],
            send_sem=(up_s if up else dn_s).at[c, d], recv_sem=(up_r if up else dn_r).at[c, d],
            device_id={"aux": z - hop if up else z + hop}, device_id_type=MESH,
        )

    def z_start(c, d):
        for up in (True, False):
            @pl.when(z_sends(d, up))
            def _():
                z_copy(c, d, up).start()

    def stage_f(c):
        for up in (True, False):
            @pl.when(z_sends(3, up))
            def _():
                z_recv(c, 2, up).wait_recv()
                z_copy(c, 3, up).start()

    def z_rest(c):
        for d in range(1, nz):
            for up in (True, False):
                here = z - d >= 0 if up else z + d < nz

                @pl.when(here & jnp.logical_not(z_sends(3, up)) if d == 2 else here)
                def _():
                    z_recv(c, d, up).wait_recv()

    def stage_a(c):
        at, step = chunks[c]
        for copy in a_copies[c]:
            copy.wait_recv()

        @pl.loop(0, kept)
        def _(k):
            acc = rcv[c][tab_ref[0, k]].astype(f32)
            for j in range(1, depth_j):
                acc = acc + rcv[c][tab_ref[j, k]].astype(f32)
            rows[z, at:at + step, pl.ds(pl.multiple_of(k * width, width), width)] = acc.astype(bf16)

        z_start(c, 2)
        z_start(c, 1)

    x_copies, y_copies, o_copies = {}, {}, {}
    tile = 256
    depth = rows.shape[-1]
    piece = 16

    def stage_v():
        vir_pass[0].wait_recv()

        @pl.loop(0, width // piece)
        def _(i):
            at = pl.ds(pl.multiple_of(i * piece, piece), piece)
            for k in range(kept):
                to = pl.ds(pl.multiple_of(k * width + i * piece, piece), piece)
                vir[to, :] = vir_both[tab_ref[most, k], at, :]

    def stage_m(c):
        at, step = chunks[c]
        mid = step // 2
        lo, hi, here = pl.ds(at, mid), pl.ds(at + mid, mid), pl.ds(at // 2, mid)

        with jax.named_scope("Z"):
            z_rest(c)

        @pl.loop(0, vir.shape[1] // tile)
        def _(j):
            cols = pl.ds(pl.multiple_of(j * tile, tile), tile)
            left = rows[:, at:at + step, :].reshape(nz * step, depth)
            got = jnp.dot(left, vir[:, cols], preferred_element_type=f32)
            part[:, at:at + step, cols] = got.astype(bf16).reshape(nz, step, tile)

        far = 2 * (1 - cy) + 1 - cx
        x_copies[c] = [
            remote(part.at[far, lo], rx.at[0, here], x_s.at[c, 0], x_r.at[c, 0], xmate),
            remote(part.at[far, hi], ry.at[0, here], y_s.at[c, 0], y_r.at[c, 0], ymate),
            remote(part.at[2 * cy + 1 - cx, lo], rx.at[1, here], x_s.at[c, 1], x_r.at[c, 1], xmate),
            remote(part.at[2 * (1 - cy) + cx, hi], ry.at[1, here], y_s.at[c, 1], y_r.at[c, 1], ymate),
        ]

    def add2(a, b):
        return (a.astype(f32) + b.astype(f32)).astype(bf16)

    def stage_x(c):
        at, step = chunks[c]
        mid = step // 2
        here, there = slice(at // 2, at // 2 + mid), pl.ds(at // 2, mid)
        for copy in x_copies[c][:2]:
            copy.wait_recv()
        tx[here] = add2(part[2 * (1 - cy) + cx, at:at + mid], rx[0, here])
        ty[here] = add2(part[2 * cy + 1 - cx, at + mid:at + step], ry[0, here])
        y_copies[c] = [
            remote(tx.at[there], rx.at[2, there], y_s.at[c, 2], y_r.at[c, 2], ymate),
            remote(ty.at[there], ry.at[2, there], x_s.at[c, 2], x_r.at[c, 2], xmate),
        ]

    def stage_y(c):
        at, step = chunks[c]
        mid = step // 2
        here = slice(at // 2, at // 2 + mid)
        for copy in x_copies[c][2:] + y_copies[c]:
            copy.wait_recv()
        top = part[chip, at:at + mid].astype(f32) + rx[1, here].astype(f32) + rx[2, here].astype(f32)
        low = part[chip, at + mid:at + step].astype(f32) + ry[1, here].astype(f32) + ry[2, here].astype(f32)
        out_ref[at:at + mid, :] = top.astype(bf16)
        out_ref[at + mid:at + step, :] = low.astype(bf16)
        o_copies[c] = pltpu.make_async_copy(out_ref.at[pl.ds(at, step)], out_hbm.at[pl.ds(at, step)], out_sem.at[c])
        o_copies[c].start()

    def stage_s(c):
        for copy in [h_copies[c]] + a_copies[c]:
            copy.wait_send()
        for d in range(1, nz):
            for up in (True, False):
                @pl.when(z_sends(d, up))
                def _():
                    z_copy(c, d, up).wait_send()

    def stage_t(c):
        for copy in x_copies[c] + y_copies[c]:
            copy.wait_send()
        o_copies[c].wait()

    run = {"H": stage_h, "P": stage_p, "W": stage_w, "A": stage_a, "F": stage_f, "M": stage_m, "X": stage_x,
           "Y": stage_y, "V": stage_v, "S": stage_s, "T": stage_t}
    for item in make_plan(count):
        with jax.named_scope(item):
            run[item[0]](*[int(v) for v in item[1:]])
    vir_pass[0].wait_send()


def fused(n, nz, sizes, call_id, tab, lhs, blocks, vir3):
    kept, depth_j, cross = sizes
    slots, deep, _, width = blocks.shape
    per_owner, _, columns = vir3.shape
    span = deep * lhs.shape[0] // slots // 4
    steps = [step for _, step in cuts(span)]
    count, cap = len(steps), 2 * slots
    dma, vm = pltpu.SemaphoreType.DMA, pltpu.VMEM
    anywhere, whole = pl.BlockSpec(memory_space=pl.ANY), pl.BlockSpec(memory_space=pltpu.VMEM)
    return pl.pallas_call(
        functools.partial(main_kernel, n, nz, kept, depth_j, cross),
        out_shape=jax.ShapeDtypeStruct((span, columns), bf16),
        in_specs=[pl.BlockSpec(memory_space=pltpu.SMEM), whole, anywhere, anywhere],
        out_specs=anywhere,
        scratch_shapes=[
            vm((span, columns), bf16), dma((count,)),
            vm((2 * per_owner, width, columns), bf16),
            vm((kept * width, columns), bf16),
            vm(blocks.shape, bf16),
            vm((slots, span, width), bf16),
            vm((3, cross, span, width), bf16),
            vm((nz, span, kept * width), bf16),
            vm((nz, span, columns), bf16),
            vm((3, span // 2, columns), bf16),
            vm((3, span // 2, columns), bf16),
            vm((span // 2, columns), bf16),
            vm((span // 2, columns), bf16),
            dma, dma, dma,
            dma((count, 2)), dma((count,)), dma((count,)),
            dma((count, 3)), dma((count, 3)),
            dma((count, nz)), dma((count, nz)), dma((count, nz)), dma((count, nz)),
            dma((count, 3)), dma((count, 3)), dma((count, 3)), dma((count, 3)),
        ] + [vm((cap, step, width), bf16) for step in steps] + [
            vm((n // 2 * cap + 1, step, width), bf16) for step in steps
        ],
        compiler_params=pltpu.CompilerParams(
            collective_id=call_id, has_side_effects=True, vmem_limit_bytes=62 * 1024 * 1024,
        ),
    )(tab, lhs, blocks, vir3)


def per_device(blocks, pairs, counts, owned_blocks, occ_coef, vir_coef):
    groups, nz = lax.axis_size("ao"), lax.axis_size("aux")
    slots, _, _, width = blocks.shape
    per_owner, occupied, _ = occ_coef.shape
    variants = VARIANTS + ((2 * per_owner, groups * CAP, 2 * slots),)
    tab, lhs, which = prepare(groups, variants, pairs, counts, owned_blocks, occ_coef)
    vir3 = vir_coef.reshape(per_owner, width, vir_coef.shape[1])
    out = lax.switch(
        which.reshape(()), [functools.partial(fused, groups, nz, v, 1 + i) for i, v in enumerate(variants)],
        tab, lhs, blocks, vir3,
    )
    return out.reshape(-1, occupied, vir_coef.shape[1])


def per_device_general(blocks, pairs, counts, owned_blocks, occ_coef, vir_coef):
    groups = lax.axis_size("ao")
    own_index = lax.axis_index("ao")
    slot_count = blocks.shape[0]
    aux_depth = blocks.shape[1]
    block_width = blocks.shape[3]
    occupied = occ_coef.shape[1]
    all_pairs, all_counts, all_owned = (
        lax.all_gather(pairs, "ao", axis=0, tiled=True),
        lax.all_gather(counts, "ao", axis=0, tiled=True),
        lax.all_gather(owned_blocks, "ao", axis=0, tiled=True),
    )
    occ_all = lax.all_gather(occ_coef, "ao", axis=0, tiled=True)
    per_owner = all_owned.shape[0] // groups
    slot_ids = jnp.arange(slot_count, dtype=jnp.int32)
    in_use = slot_ids < counts[0]
    occ_pick = occ_all[block_place(pairs[:, 0], all_owned)]
    slab_values = jnp.einsum("sim,spmn->spin", occ_pick, blocks, preferred_element_type=jnp.float32)
    slab_values = jnp.where(in_use[:, None, None, None], slab_values, 0.0).astype(jnp.bfloat16)
    flat_slabs = slab_values.reshape(slot_count, aux_depth * occupied, block_width)
    place_all = block_place(all_pairs[:, 1], all_owned).reshape(groups, slot_count)
    owner_all = place_all // per_owner
    local_all = place_all % per_owner
    live_all = slot_ids[None, :] < all_counts[:, None]
    mine_all = live_all & (owner_all == own_index)
    local_ids = jnp.arange(per_owner, dtype=jnp.int32)
    slabs_got = lax.all_gather(flat_slabs, "ao", axis=0, tiled=True)
    assign = (
        mine_all.reshape(-1)[None, :] & (local_all.reshape(-1)[None, :] == local_ids[:, None])
    ).astype(jnp.bfloat16)
    summed = jnp.einsum("lt,tqm->qlm", assign, slabs_got, preferred_element_type=jnp.float32)
    rows_local = summed.reshape(summed.shape[0], per_owner * block_width).astype(jnp.bfloat16)
    rows_whole = lax.all_gather(rows_local, "aux", axis=0, tiled=True)
    share = rows_whole.shape[0] // groups
    result = lax.psum_scatter(
        jnp.dot(rows_whole, vir_coef, preferred_element_type=jnp.float32).astype(jnp.bfloat16),
        "ao",
        scatter_dimension=0,
        tiled=True,
    )
    return result.reshape(share // occupied, occupied, vir_coef.shape[1])


def solution(mesh):
    in_specs = (
        P("ao", "aux", None, None),
        P("ao", None),
        P("ao"),
        P("ao"),
        P("ao", None, None),
        P("ao", "aux"),
    )
    out_specs = P("ao", None, "aux")
    small = mesh.shape["ao"] == 8 and mesh.shape["aux"] == 4
    body = per_device if small else per_device_general
    return jax.shard_map(body, mesh=mesh, in_specs=in_specs, out_specs=out_specs, check_vma=False)
```

time: 92.8 us -> 77 us (0.83)
  Pallas kernels: 89.8 us -> 74.2 us
    pallas_call x1, Pallas kernels: 73.6 us -> 65.3 us  [fused(): pl.pallas_call(functools.partial(main_kernel, n, nz, kept, depth_j, cross...]
    pallas_call x1, Pallas kernels: 16.1 us -> 8.89 us  [prepare(): pl.pallas_call(functools.partial(prep_kernel, n, variants), out_shape=(ja...]
where the time goes in v2:
time: 77 us; the launch traced here: 76.9 us
  Pallas kernels  74.2 us (96%)
  between operations  1.36 us (2%)
  local copies, waits for them, and re-layouts  1.02 us (1%)
    pallas_call x1, Pallas kernels, fused(): pl.pallas_call(functools.partial(main_kernel, n, nz, kept, depth_j, cross...  65.3 us
    pallas_call x1, Pallas kernels, prepare(): pl.pallas_call(functools.partial(prep_kernel, n, variants), out_shape=(ja...  8.89 us

profile of v2, /device:TPU:0, one launch (start us, length us, event | category | flops | bytes accessed | tf_op | source)
XLA Modules:
  0.0 76.9 jit_solution(3892873552011103430)
XLA Ops:
  0.7 8.9 %shard_map.69 = (s32[32,128]{1,0:T(8,128)S(1)}, bf16[96,256]{1,0:T(8,128)(2,1)S(1)}, s32[1,1]{1,0:T(1,128)}) custom-call(s32[2,6]{1,0:T(2,128)} %bitcast.23, s32[1,1]{1,0:T(1,128)} %bitcast.11.counts_hbm, s32[1,10]{1,0:T(1,128)} %bitcast.24, bf16[80,128]{1,0:T(8,128)(2,1)} %bitcast.22), custom_call_target="tpu_custom_call" | custom-call | tf_op jit(solution)/shard_map/pallas_call | solution.py:171
  10.2 65.6 %conditional.1 = (bf16[32,8,2304]{2,1,0:T(8,128)(2,1)S(1)}) conditional(s32[]{:T(128)} %bitcast.9, (s32[32,128]{1,0:T(8,128)S(1)}, bf16[96,256]{1,0:T(8,128)(2,1)S(1)}, bf16[6,64,128,128]{3,2,1,0:T(8,128)(2,1)}, bf16[10,128,2304]{2,1,0:T(8,128)(2,1)}) %tuple.36, (s32[32,128]{1,0:T(8,128)S(1)}, ...), branch_computations={%region_0.0_spmd, %region_1.0_spmd, %region_2.0_spmd, %region_3.0_... | conditional | bytes 8 | solution.py:511
  10.3 65.3 %branch_0_fun.1 = bf16[256,2304]{1,0:T(8,128)(2,1)S(1)} custom-call(s32[32,128]{1,0:T(8,128)S(1)} %get-tuple-element.50.tab_ref, bf16[96,256]{1,0:T(8,128)(2,1)S(1)} %get-tuple-element.52.lhs_ref, bf16[6,64,128,128]{3,2,1,0:T(8,128)(2,1)} %get-tuple-element.54.blk_hbm, bf16[10,128,2304]{2,1,0:T(8,128)(2,1)} %get-tuple-element.55.vir_hbm), custom_call_target="tpu_custom_call" | custom-call | tf_op jit(solution)/shard_map/cond/branch_0_fun/pallas_call | solution.py:472
  75.8 1.0 %copy.19 = bf16[32,8,2304]{2,1,0:T(8,128)(2,1)} copy(bf16[32,8,2304]{2,1,0:T(8,128)(2,1)S(1)} %get-tuple-element.78) | data formatting | bytes 2359296
